TPU v7x, 32 devices: a whole 2x2x4 slice. The times are simulated.
32 devices in a mesh: mkt: 8 (over y, x, core), trade: 1, scen: 4 (over z).
Axes of the slice: x: 2, y: 2, z: 4, core: 2. Of those that a mesh axis runs over, the one named last changes fastest.
Arguments:
- quotes: bfloat16 [512, 512], P('mkt'), may hold values from -6 to 6
- kernel: bfloat16 [64, 128, 128], P(('trade', 'scen')), may hold values from -0.5 to 0.5
- trade_block: int32 [2048], P('trade'), may hold values from 0 to 63
- trade_embed: bfloat16 [2048, 256], P('trade'), may hold values from -6 to 6
- position: float32 [2048], P('trade'), may hold values from -0.125 to 0.125
- scen_rank: int32 [512], P(('mkt', 'scen')), may hold values from 0 to 511, each once
- w_in: bfloat16 [128, 256], replicated, may hold values from -0.5 to 0.5
- w_mid: bfloat16 [256, 256], replicated, may hold values from -0.375 to 0.375
- b_mid: float32 [256], replicated, may hold values from -6 to 6
- w_out: bfloat16 [256], replicated, may hold values from -0.375 to 0.375
Outputs:
- book_pnl: float32 [512], P(('mkt', 'scen'))
- marginal: float32 [2048], P('trade')
- shortfall: float32 [], replicated
Inputs may be any that keep to these rules, and one draw needn't show every extreme that they name: scen_rank holds each rank of 0 to 511 once.
All inputs are finite; a program needn't handle non-finite values.
Results may differ from a plain program's by a relative error of at most 0.014.
The roundings to bfloat16 on the way count: a program that leaves them out, or rounds other values in their place, can miss the bound.
Values may be sent and summed in bfloat16 or wider, within the bound.
No kernel may reach another device: no remote copies, remote signals or barrier semaphores. Data moves between devices by JAX's collectives and lax.ppermute only.
A program may use at most 64 MiB of HBM per device.

v0:
```python
import jax
import jax.numpy as jnp
from jax import lax
from jax.sharding import PartitionSpec as P

SEG = 128
WIN = 128
QSTEP = 8


def local(quotes, kernel, trade_block, trade_embed, position, scen_rank, w_in, w_mid, b_mid, w_out):
    local_count = kernel.shape[0]
    quote_count = quotes.shape[1]
    row_count = quotes.shape[0]
    first_block = lax.axis_index(("trade", "scen")) * local_count

    def cut_window(local_block):
        block_index = first_block + local_block
        window_start = jnp.clip(QSTEP * block_index - (WIN - QSTEP) // 2, 0, quote_count - WIN)
        return lax.dynamic_slice_in_dim(quotes, window_start, WIN, 1)

    windows = jax.vmap(cut_window)(jnp.arange(local_count, dtype=jnp.int32))
    built_state = jnp.einsum("jrw,jws->jrs", windows, kernel, preferred_element_type=jnp.float32)
    built_state = built_state.astype(jnp.bfloat16).reshape(local_count, row_count * SEG)
    scen_count = scen_rank.shape[0]
    quarter = lax.all_to_all(built_state, "scen", split_axis=1, concat_axis=0, tiled=True)
    table = lax.all_gather(quarter, "trade", axis=0, tiled=True)
    trade_rows_all = table[trade_block]
    embed_float = trade_embed.astype(jnp.float32)

    def price(scen_index):
        trade_rows = lax.dynamic_slice_in_dim(trade_rows_all, scen_index * SEG, SEG, 1)
        hidden_one = jax.nn.silu(
            jnp.dot(trade_rows, w_in, preferred_element_type=jnp.float32) + embed_float
        ).astype(jnp.bfloat16)
        hidden_two = jax.nn.silu(
            jnp.dot(hidden_one, w_mid, preferred_element_type=jnp.float32) + b_mid
        ).astype(jnp.bfloat16)
        return jnp.dot(hidden_two, w_out, preferred_element_type=jnp.float32)

    values = lax.map(price, jnp.arange(scen_count, dtype=jnp.int32))
    scen_total = scen_count * lax.axis_size("mkt") * lax.axis_size("scen")
    decay_span = scen_total // 20
    weight_sum = jnp.sum(jnp.exp(-jnp.arange(scen_total, dtype=jnp.float32) / decay_span))
    weights = jnp.exp(-scen_rank.astype(jnp.float32) / decay_span) / weight_sum
    pnl_part = jnp.dot(values, position, precision=lax.Precision.HIGHEST)
    marginal = lax.psum(-jnp.dot(weights, values, precision=lax.Precision.HIGHEST), ("mkt", "scen"))
    book_pnl = lax.psum(pnl_part, "trade")
    local_tail = -jnp.dot(weights, book_pnl, precision=lax.Precision.HIGHEST)
    shortfall = lax.psum(local_tail, ("mkt", "scen"))
    return (book_pnl, marginal, shortfall)


def solution(mesh):
    placed = (
        P("mkt", None),
        P(("trade", "scen"), None, None),
        P("trade"),
        P("trade", None),
        P("trade"),
        P(("mkt", "scen")),
        P(),
        P(),
        P(),
        P(),
    )
    return jax.shard_map(
        local,
        mesh=mesh,
        in_specs=placed,
        out_specs=(P(("mkt", "scen")), P("trade"), P()),
        check_vma=False,
    )
```

profile of v0, /device:TPU:0, one launch (start us, length us, event | category | flops | bytes accessed | tf_op | source)
XLA Modules:
  0.0 204.2 jit_solution(12396054698393962323)
XLA Ops:
  0.7 33.3 %while.12 = (s32[]{:T(128)}, bf16[64,512]{1,0:T(8,128)(2,1)}, s32[16,2]{0,1:T(2,128)S(1)}, bf16[16,64,128]{2,1,0:T(8,128)(2,1)S(1)}, s32[]{:T(128)}) while((s32[]{:T(128)}, bf16[64,512]{1,0:T(8,128)(2,1)}, s32[16,2]{0,1:T(2,128)S(1)}, bf16[16,64,128]{2,1,0:T(8,128)(2,1)S(1)}, s32[]{:T(128)}) %tuple.34), condition=%wide.while_cond, body=%wide.while_body.sunk | while | flops 2 | bytes 32865 | solution.py:20
  35.2 6.0 %all-to-all-start = ((bf16[16,4,2048]{2,0,1:T(8,128)(2,1)}), bf16[16,4,2048]{2,0,1:T(8,128)(2,1)S(1)}, u32[]{:S(2)}, u32[]{:S(2)}) async-start(bf16[16,4,2048]{2,0,1:T(8,128)(2,1)} %copy.14), calls=%async_computation | async-start | bytes 524288 | tf_op jit(solution)/shard_map/all_to_all | solution.py:26
  43.2 6.9 %all-to-all-done = bf16[16,4,2048]{2,0,1:T(8,128)(2,1)S(1)} async-done(((bf16[16,4,2048]{2,0,1:T(8,128)(2,1)}), bf16[16,4,2048]{2,0,1:T(8,128)(2,1)S(1)}, u32[]{:S(2)}, u32[]{:S(2)}) %all-to-all-start) | async-done | bytes 262176 | tf_op jit(solution)/shard_map/all_to_all | solution.py:26
  50.2 11.0 %gather_fusion = bf16[2048,2048]{1,0:T(8,128)(2,1)} fusion(bf16[64,2048]{1,0:T(8,128)(2,1)S(1)} %bitcast.38, s32[2048]{0:T(1024)S(1)} %fusion.6), kind=kCustom, calls=%fused_computation | custom fusion | bytes 16785408 | tf_op jit(solution)/shard_map/gather | solution.py:28
  61.2 100.5 %while.11 = (s32[]{:T(128)}, f32[16,2048]{1,0:T(8,128)S(1)}, s32[16]{0:T(128)S(1)}, bf16[2048,2048]{1,0:T(8,128)(2,1)}, bf16[128,256]{1,0:T(8,128)(2,1)S(1)}, /*...) while((s32[]{:T(128)}, f32[16,2048]{1,0:T(8,128)S(1)}, ...), condition=%wide.region_1.2_spmd, body=%wide.region_0.1_spmd.sunk | while | flops 409993216 | bytes 4942527 | solution.py:41
  62.4 2.8 %multiply_convert_fusion.3 = bf16[2048,256]{1,0:T(8,128)(2,1)} fusion(f32[2048,256]{1,0:T(8,128)S(1)} %get-tuple-element.215, bf16[128,256]{1,0:T(8,128)(2,1)S(1)} %get-tuple-element.214, bf16[2048,2048]{1,0:T(8,128)(2,1)} %get-tuple-element.213, s32[]{:T(128)S(6)} %select_n.23), kind=kOutput, calls=%fused_computation.4.clone.1 | convolution fusion | flops 137363456 | bytes 3735556 | tf_op jit(solution)/shard_map/while/body/eval_jaxpr/dot_general | solution.py:34
  65.2 2.0 %fusion.29 = f32[1,2048]{1,0:T(1,128)S(1)} fusion(bf16[256,1]{0,1:T(2,128)(2,1)S(1)} %reshape.77, bf16[2048,256]{1,0:T(8,128)(2,1)} %multiply_convert_fusion.3, bf16[256,256]{1,0:T(8,128)(2,1)S(1)} %get-tuple-element.216, f32[256]{0:T(256)S(1)} %get-tuple-element.217), kind=kOutput, calls=%fused_computation.5.clone.1 | convolution fusion | flops 272629760 | bytes 1189376 | tf_op jit(solution)/shard_map/while/body/eval_jaxpr/dot_general | solution.py:39
  68.7 2.8 %multiply_convert_fusion.3 = bf16[2048,256]{1,0:T(8,128)(2,1)} fusion(f32[2048,256]{1,0:T(8,128)S(1)} %get-tuple-element.215, bf16[128,256]{1,0:T(8,128)(2,1)S(1)} %get-tuple-element.214, bf16[2048,2048]{1,0:T(8,128)(2,1)} %get-tuple-element.213, s32[]{:T(128)S(6)} %select_n.23), kind=kOutput, calls=%fused_computation.4.clone.1 | convolution fusion | flops 137363456 | bytes 3735556 | tf_op jit(solution)/shard_map/while/body/eval_jaxpr/dot_general | solution.py:34
  71.5 2.0 %fusion.29 = f32[1,2048]{1,0:T(1,128)S(1)} fusion(bf16[256,1]{0,1:T(2,128)(2,1)S(1)} %reshape.77, bf16[2048,256]{1,0:T(8,128)(2,1)} %multiply_convert_fusion.3, bf16[256,256]{1,0:T(8,128)(2,1)S(1)} %get-tuple-element.216, f32[256]{0:T(256)S(1)} %get-tuple-element.217), kind=kOutput, calls=%fused_computation.5.clone.1 | convolution fusion | flops 272629760 | bytes 1189376 | tf_op jit(solution)/shard_map/while/body/eval_jaxpr/dot_general | solution.py:39
  75.0 2.8 %multiply_convert_fusion.3 = bf16[2048,256]{1,0:T(8,128)(2,1)} fusion(f32[2048,256]{1,0:T(8,128)S(1)} %get-tuple-element.215, bf16[128,256]{1,0:T(8,128)(2,1)S(1)} %get-tuple-element.214, bf16[2048,2048]{1,0:T(8,128)(2,1)} %get-tuple-element.213, s32[]{:T(128)S(6)} %select_n.23), kind=kOutput, calls=%fused_computation.4.clone.1 | convolution fusion | flops 137363456 | bytes 3735556 | tf_op jit(solution)/shard_map/while/body/eval_jaxpr/dot_general | solution.py:34
  77.8 2.0 %fusion.29 = f32[1,2048]{1,0:T(1,128)S(1)} fusion(bf16[256,1]{0,1:T(2,128)(2,1)S(1)} %reshape.77, bf16[2048,256]{1,0:T(8,128)(2,1)} %multiply_convert_fusion.3, bf16[256,256]{1,0:T(8,128)(2,1)S(1)} %get-tuple-element.216, f32[256]{0:T(256)S(1)} %get-tuple-element.217), kind=kOutput, calls=%fused_computation.5.clone.1 | convolution fusion | flops 272629760 | bytes 1189376 | tf_op jit(solution)/shard_map/while/body/eval_jaxpr/dot_general | solution.py:39
  81.3 2.8 %multiply_convert_fusion.3 = bf16[2048,256]{1,0:T(8,128)(2,1)} fusion(f32[2048,256]{1,0:T(8,128)S(1)} %get-tuple-element.215, bf16[128,256]{1,0:T(8,128)(2,1)S(1)} %get-tuple-element.214, bf16[2048,2048]{1,0:T(8,128)(2,1)} %get-tuple-element.213, s32[]{:T(128)S(6)} %select_n.23), kind=kOutput, calls=%fused_computation.4.clone.1 | convolution fusion | flops 137363456 | bytes 3735556 | tf_op jit(solution)/shard_map/while/body/eval_jaxpr/dot_general | solution.py:34
  84.1 2.0 %fusion.29 = f32[1,2048]{1,0:T(1,128)S(1)} fusion(bf16[256,1]{0,1:T(2,128)(2,1)S(1)} %reshape.77, bf16[2048,256]{1,0:T(8,128)(2,1)} %multiply_convert_fusion.3, bf16[256,256]{1,0:T(8,128)(2,1)S(1)} %get-tuple-element.216, f32[256]{0:T(256)S(1)} %get-tuple-element.217), kind=kOutput, calls=%fused_computation.5.clone.1 | convolution fusion | flops 272629760 | bytes 1189376 | tf_op jit(solution)/shard_map/while/body/eval_jaxpr/dot_general | solution.py:39
  87.6 2.8 %multiply_convert_fusion.3 = bf16[2048,256]{1,0:T(8,128)(2,1)} fusion(f32[2048,256]{1,0:T(8,128)S(1)} %get-tuple-element.215, bf16[128,256]{1,0:T(8,128)(2,1)S(1)} %get-tuple-element.214, bf16[2048,2048]{1,0:T(8,128)(2,1)} %get-tuple-element.213, s32[]{:T(128)S(6)} %select_n.23), kind=kOutput, calls=%fused_computation.4.clone.1 | convolution fusion | flops 137363456 | bytes 3735556 | tf_op jit(solution)/shard_map/while/body/eval_jaxpr/dot_general | solution.py:34
  90.4 2.0 %fusion.29 = f32[1,2048]{1,0:T(1,128)S(1)} fusion(bf16[256,1]{0,1:T(2,128)(2,1)S(1)} %reshape.77, bf16[2048,256]{1,0:T(8,128)(2,1)} %multiply_convert_fusion.3, bf16[256,256]{1,0:T(8,128)(2,1)S(1)} %get-tuple-element.216, f32[256]{0:T(256)S(1)} %get-tuple-element.217), kind=kOutput, calls=%fused_computation.5.clone.1 | convolution fusion | flops 272629760 | bytes 1189376 | tf_op jit(solution)/shard_map/while/body/eval_jaxpr/dot_general | solution.py:39
  93.8 2.8 %multiply_convert_fusion.3 = bf16[2048,256]{1,0:T(8,128)(2,1)} fusion(f32[2048,256]{1,0:T(8,128)S(1)} %get-tuple-element.215, bf16[128,256]{1,0:T(8,128)(2,1)S(1)} %get-tuple-element.214, bf16[2048,2048]{1,0:T(8,128)(2,1)} %get-tuple-element.213, s32[]{:T(128)S(6)} %select_n.23), kind=kOutput, calls=%fused_computation.4.clone.1 | convolution fusion | flops 137363456 | bytes 3735556 | tf_op jit(solution)/shard_map/while/body/eval_jaxpr/dot_general | solution.py:34
  96.6 2.0 %fusion.29 = f32[1,2048]{1,0:T(1,128)S(1)} fusion(bf16[256,1]{0,1:T(2,128)(2,1)S(1)} %reshape.77, bf16[2048,256]{1,0:T(8,128)(2,1)} %multiply_convert_fusion.3, bf16[256,256]{1,0:T(8,128)(2,1)S(1)} %get-tuple-element.216, f32[256]{0:T(256)S(1)} %get-tuple-element.217), kind=kOutput, calls=%fused_computation.5.clone.1 | convolution fusion | flops 272629760 | bytes 1189376 | tf_op jit(solution)/shard_map/while/body/eval_jaxpr/dot_general | solution.py:39
  100.1 2.8 %multiply_convert_fusion.3 = bf16[2048,256]{1,0:T(8,128)(2,1)} fusion(f32[2048,256]{1,0:T(8,128)S(1)} %get-tuple-element.215, bf16[128,256]{1,0:T(8,128)(2,1)S(1)} %get-tuple-element.214, bf16[2048,2048]{1,0:T(8,128)(2,1)} %get-tuple-element.213, s32[]{:T(128)S(6)} %select_n.23), kind=kOutput, calls=%fused_computation.4.clone.1 | convolution fusion | flops 137363456 | bytes 3735556 | tf_op jit(solution)/shard_map/while/body/eval_jaxpr/dot_general | solution.py:34
  102.9 2.0 %fusion.29 = f32[1,2048]{1,0:T(1,128)S(1)} fusion(bf16[256,1]{0,1:T(2,128)(2,1)S(1)} %reshape.77, bf16[2048,256]{1,0:T(8,128)(2,1)} %multiply_convert_fusion.3, bf16[256,256]{1,0:T(8,128)(2,1)S(1)} %get-tuple-element.216, f32[256]{0:T(256)S(1)} %get-tuple-element.217), kind=kOutput, calls=%fused_computation.5.clone.1 | convolution fusion | flops 272629760 | bytes 1189376 | tf_op jit(solution)/shard_map/while/body/eval_jaxpr/dot_general | solution.py:39
  106.4 2.8 %multiply_convert_fusion.3 = bf16[2048,256]{1,0:T(8,128)(2,1)} fusion(f32[2048,256]{1,0:T(8,128)S(1)} %get-tuple-element.215, bf16[128,256]{1,0:T(8,128)(2,1)S(1)} %get-tuple-element.214, bf16[2048,2048]{1,0:T(8,128)(2,1)} %get-tuple-element.213, s32[]{:T(128)S(6)} %select_n.23), kind=kOutput, calls=%fused_computation.4.clone.1 | convolution fusion | flops 137363456 | bytes 3735556 | tf_op jit(solution)/shard_map/while/body/eval_jaxpr/dot_general | solution.py:34
  109.2 2.0 %fusion.29 = f32[1,2048]{1,0:T(1,128)S(1)} fusion(bf16[256,1]{0,1:T(2,128)(2,1)S(1)} %reshape.77, bf16[2048,256]{1,0:T(8,128)(2,1)} %multiply_convert_fusion.3, bf16[256,256]{1,0:T(8,128)(2,1)S(1)} %get-tuple-element.216, f32[256]{0:T(256)S(1)} %get-tuple-element.217), kind=kOutput, calls=%fused_computation.5.clone.1 | convolution fusion | flops 272629760 | bytes 1189376 | tf_op jit(solution)/shard_map/while/body/eval_jaxpr/dot_general | solution.py:39
  112.7 2.8 %multiply_convert_fusion.3 = bf16[2048,256]{1,0:T(8,128)(2,1)} fusion(f32[2048,256]{1,0:T(8,128)S(1)} %get-tuple-element.215, bf16[128,256]{1,0:T(8,128)(2,1)S(1)} %get-tuple-element.214, bf16[2048,2048]{1,0:T(8,128)(2,1)} %get-tuple-element.213, s32[]{:T(128)S(6)} %select_n.23), kind=kOutput, calls=%fused_computation.4.clone.1 | convolution fusion | flops 137363456 | bytes 3735556 | tf_op jit(solution)/shard_map/while/body/eval_jaxpr/dot_general | solution.py:34
  119.0 2.8 %multiply_convert_fusion.3 = bf16[2048,256]{1,0:T(8,128)(2,1)} fusion(f32[2048,256]{1,0:T(8,128)S(1)} %get-tuple-element.215, bf16[128,256]{1,0:T(8,128)(2,1)S(1)} %get-tuple-element.214, bf16[2048,2048]{1,0:T(8,128)(2,1)} %get-tuple-element.213, s32[]{:T(128)S(6)} %select_n.23), kind=kOutput, calls=%fused_computation.4.clone.1 | convolution fusion | flops 137363456 | bytes 3735556 | tf_op jit(solution)/shard_map/while/body/eval_jaxpr/dot_general | solution.py:34
  121.8 2.0 %fusion.29 = f32[1,2048]{1,0:T(1,128)S(1)} fusion(bf16[256,1]{0,1:T(2,128)(2,1)S(1)} %reshape.77, bf16[2048,256]{1,0:T(8,128)(2,1)} %multiply_convert_fusion.3, bf16[256,256]{1,0:T(8,128)(2,1)S(1)} %get-tuple-element.216, f32[256]{0:T(256)S(1)} %get-tuple-element.217), kind=kOutput, calls=%fused_computation.5.clone.1 | convolution fusion | flops 272629760 | bytes 1189376 | tf_op jit(solution)/shard_map/while/body/eval_jaxpr/dot_general | solution.py:39
  125.2 2.8 %multiply_convert_fusion.3 = bf16[2048,256]{1,0:T(8,128)(2,1)} fusion(f32[2048,256]{1,0:T(8,128)S(1)} %get-tuple-element.215, bf16[128,256]{1,0:T(8,128)(2,1)S(1)} %get-tuple-element.214, bf16[2048,2048]{1,0:T(8,128)(2,1)} %get-tuple-element.213, s32[]{:T(128)S(6)} %select_n.23), kind=kOutput, calls=%fused_computation.4.clone.1 | convolution fusion | flops 137363456 | bytes 3735556 | tf_op jit(solution)/shard_map/while/body/eval_jaxpr/dot_general | solution.py:34
  128.0 2.0 %fusion.29 = f32[1,2048]{1,0:T(1,128)S(1)} fusion(bf16[256,1]{0,1:T(2,128)(2,1)S(1)} %reshape.77, bf16[2048,256]{1,0:T(8,128)(2,1)} %multiply_convert_fusion.3, bf16[256,256]{1,0:T(8,128)(2,1)S(1)} %get-tuple-element.216, f32[256]{0:T(256)S(1)} %get-tuple-element.217), kind=kOutput, calls=%fused_computation.5.clone.1 | convolution fusion | flops 272629760 | bytes 1189376 | tf_op jit(solution)/shard_map/while/body/eval_jaxpr/dot_general | solution.py:39
  131.5 2.8 %multiply_convert_fusion.3 = bf16[2048,256]{1,0:T(8,128)(2,1)} fusion(f32[2048,256]{1,0:T(8,128)S(1)} %get-tuple-element.215, bf16[128,256]{1,0:T(8,128)(2,1)S(1)} %get-tuple-element.214, bf16[2048,2048]{1,0:T(8,128)(2,1)} %get-tuple-element.213, s32[]{:T(128)S(6)} %select_n.23), kind=kOutput, calls=%fused_computation.4.clone.1 | convolution fusion | flops 137363456 | bytes 3735556 | tf_op jit(solution)/shard_map/while/body/eval_jaxpr/dot_general | solution.py:34
  137.8 2.8 %multiply_convert_fusion.3 = bf16[2048,256]{1,0:T(8,128)(2,1)} fusion(f32[2048,256]{1,0:T(8,128)S(1)} %get-tuple-element.215, bf16[128,256]{1,0:T(8,128)(2,1)S(1)} %get-tuple-element.214, bf16[2048,2048]{1,0:T(8,128)(2,1)} %get-tuple-element.213, s32[]{:T(128)S(6)} %select_n.23), kind=kOutput, calls=%fused_computation.4.clone.1 | convolution fusion | flops 137363456 | bytes 3735556 | tf_op jit(solution)/shard_map/while/body/eval_jaxpr/dot_general | solution.py:34
  144.1 2.8 %multiply_convert_fusion.3 = bf16[2048,256]{1,0:T(8,128)(2,1)} fusion(f32[2048,256]{1,0:T(8,128)S(1)} %get-tuple-element.215, bf16[128,256]{1,0:T(8,128)(2,1)S(1)} %get-tuple-element.214, bf16[2048,2048]{1,0:T(8,128)(2,1)} %get-tuple-element.213, s32[]{:T(128)S(6)} %select_n.23), kind=kOutput, calls=%fused_computation.4.clone.1 | convolution fusion | flops 137363456 | bytes 3735556 | tf_op jit(solution)/shard_map/while/body/eval_jaxpr/dot_general | solution.py:34
  150.4 2.8 %multiply_convert_fusion.3 = bf16[2048,256]{1,0:T(8,128)(2,1)} fusion(f32[2048,256]{1,0:T(8,128)S(1)} %get-tuple-element.215, bf16[128,256]{1,0:T(8,128)(2,1)S(1)} %get-tuple-element.214, bf16[2048,2048]{1,0:T(8,128)(2,1)} %get-tuple-element.213, s32[]{:T(128)S(6)} %select_n.23), kind=kOutput, calls=%fused_computation.4.clone.1 | convolution fusion | flops 137363456 | bytes 3735556 | tf_op jit(solution)/shard_map/while/body/eval_jaxpr/dot_general | solution.py:34
  156.7 2.8 %multiply_convert_fusion.3 = bf16[2048,256]{1,0:T(8,128)(2,1)} fusion(f32[2048,256]{1,0:T(8,128)S(1)} %get-tuple-element.215, bf16[128,256]{1,0:T(8,128)(2,1)S(1)} %get-tuple-element.214, bf16[2048,2048]{1,0:T(8,128)(2,1)} %get-tuple-element.213, s32[]{:T(128)S(6)} %select_n.23), kind=kOutput, calls=%fused_computation.4.clone.1 | convolution fusion | flops 137363456 | bytes 3735556 | tf_op jit(solution)/shard_map/while/body/eval_jaxpr/dot_general | solution.py:34
  165.3 39.0 %all-reduce.1 = (f32[2048]{0:T(1024)}, f32[]{:T(128)}) all-reduce(f32[2048]{0:T(1024)S(1)} %neg.21, f32[]{:T(128)S(6)} %neg.22), channel_id=1, replica_groups=mesh['mkt'=8,'trade'=1,'scen'=4] {'mkt','scen'}, use_global_device_ids=true, to_apply=%region_3.4 | all-reduce | flops 2049 | bytes 16392 | tf_op jit(solution)/shard_map/psum | solution.py:47
  (132 shorter events, 63.9 us)
Async XLA Ops:
  0.6 33.4 %copy-start = (bf16[16,128,128]{2,1,0:T(8,128)(2,1)S(1)}, bf16[16,128,128]{2,1,0:T(8,128)(2,1)}, u32[]{:S(2)}) copy-start(bf16[16,128,128]{2,1,0:T(8,128)(2,1)} %param.13) | copy-start | bytes 1572868
  34.4 8.9 %copy-start.2 = (s32[2048]{0:T(1024)S(1)}, s32[2048]{0:T(1024)}, u32[]{:S(2)}) copy-start(s32[2048]{0:T(1024)} %param.14) | copy-start | bytes 24580
  35.2 14.9 %all-to-all-start = ((bf16[16,4,2048]{2,0,1:T(8,128)(2,1)}), bf16[16,4,2048]{2,0,1:T(8,128)(2,1)S(1)}, u32[]{:S(2)}, u32[]{:S(2)}) async-start(bf16[16,4,2048]{2,0,1:T(8,128)(2,1)} %copy.14), calls=%async_computation | async-start | bytes 524288 | tf_op jit(solution)/shard_map/all_to_all | solution.py:26
  50.1 11.0 %copy-start.4 = (bf16[256,256]{1,0:T(8,128)(2,1)S(1)}, bf16[256,256]{1,0:T(8,128)(2,1)}, u32[]{:S(2)}) copy-start(bf16[256,256]{1,0:T(8,128)(2,1)} %param.19) | copy-start | bytes 393220
  50.1 11.0 %copy-start.5 = (bf16[128,256]{1,0:T(8,128)(2,1)S(1)}, bf16[128,256]{1,0:T(8,128)(2,1)}, u32[]{:S(2)}) copy-start(bf16[128,256]{1,0:T(8,128)(2,1)} %param.18) | copy-start | bytes 196612
  50.1 11.0 %copy-start.6 = (f32[256]{0:T(256)S(1)}, f32[256]{0:T(256)}, u32[]{:S(2)}) copy-start(f32[256]{0:T(256)} %param.20) | copy-start | bytes 3076
  50.2 11.0 %copy-start.7 = (bf16[256]{0:T(256)(128)(2,1)S(1)}, bf16[256]{0:T(256)(128)(2,1)}, u32[]{:S(2)}) copy-start(bf16[256]{0:T(256)(128)(2,1)} %param.21) | copy-start | bytes 1540
  61.1 100.6 %copy-start.3 = (s32[16]{0:T(128)S(1)}, s32[16]{0:T(128)}, u32[]{:S(2)}) copy-start(s32[16]{0:T(128)} %param.17) | copy-start | bytes 196
  61.2 101.4 %copy-start.1 = (f32[2048]{0:T(1024)S(1)}, f32[2048]{0:T(1024)}, u32[]{:S(2)}) copy-start(f32[2048]{0:T(1024)} %param.16) | copy-start | bytes 24580
where the time goes:
time: 207 us; the launch traced here: 204 us
  matrix products  80.6 us (39%)
  local copies, waits for them, and re-layouts  57.4 us (28%)
  blocking collectives  39 us (19%)
  loops' own time  10.9 us (5%)
  waiting for transfers between devices  6.9 us (3%)
  starting transfers between devices  6.02 us (3%)
    dot_general x16, matrix products, price(): jnp.dot(trade_rows, w_in, preferred_element_type=jnp.float32) + embed_float  44.7 us
    psum x1, blocking collectives, local(): lax.psum(-jnp.dot(weights, values, precision=lax.Precision.HIGHEST), ('mk...  39 us
    gather x48, local copies, waits for them, and re-layouts  33.3 us
    dot_general x16, matrix products, price(): return jnp.dot(hidden_two, w_out, preferred_element_type=jnp.float32)  32.7 us
    gather x1, local copies, waits for them, and re-layouts, local(): trade_rows_all = table[trade_block]  11 us
    another operation x1, loops' own time, local(): values = lax.map(price, jnp.arange(scen_count, dtype=jnp.int32))  10.9 us
    dynamic_slice x16, local copies, waits for them, and re-layouts, local(): values = lax.map(price, jnp.arange(scen_count, dtype=jnp.int32))  9.38 us
    all_to_all x1, waiting for transfers between devices, local(): lax.all_to_all(built_state, 'scen', split_axis=1, concat_axis=0, tiled=True)  6.9 us
  transfers between devices with their start and end apart: 1, of which 1 were waited for; matrix products, arithmetic and copies ran while one was open for 1% of the time, Pallas kernels for 0%

commit v1 on v0

--- a/solution.py
+++ b/solution.py
@@ -44,7 +44,8 @@
     weight_sum = jnp.sum(jnp.exp(-jnp.arange(scen_total, dtype=jnp.float32) / decay_span))
     weights = jnp.exp(-scen_rank.astype(jnp.float32) / decay_span) / weight_sum
     pnl_part = jnp.dot(values, position, precision=lax.Precision.HIGHEST)
-    marginal = lax.psum(-jnp.dot(weights, values, precision=lax.Precision.HIGHEST), ("mkt", "scen"))
+    half = lax.psum(-jnp.dot(weights, values, precision=lax.Precision.HIGHEST), "scen")
+    marginal = lax.psum(half, "mkt")
     book_pnl = lax.psum(pnl_part, "trade")
     local_tail = -jnp.dot(weights, book_pnl, precision=lax.Precision.HIGHEST)
     shortfall = lax.psum(local_tail, ("mkt", "scen"))

time: 207 us -> 231 us (1.12)
  blocking collectives: 39 us -> 61.8 us
    psum x1 -> x3, blocking collectives: 39 us -> 61.8 us  [the longest x1 38.8 us: local(): shortfall = lax.psum(local_tail, ('mkt', 'scen'))]
where the time goes in v1:
time: 231 us; the launch traced here: 228 us
  matrix products  81 us (35%)
  blocking collectives  61.8 us (27%)
  local copies, waits for them, and re-layouts  57.4 us (25%)
  loops' own time  10.9 us (5%)
  waiting for transfers between devices  6.9 us (3%)
  starting transfers between devices  6.02 us (3%)
    dot_general x16, matrix products, price(): jnp.dot(trade_rows, w_in, preferred_element_type=jnp.float32) + embed_float  45.2 us
    psum x1, blocking collectives, local(): shortfall = lax.psum(local_tail, ('mkt', 'scen'))  38.8 us
    gather x48, local copies, waits for them, and re-layouts  33.3 us
    dot_general x16, matrix products, price(): return jnp.dot(hidden_two, w_out, preferred_element_type=jnp.float32)  32.7 us
    psum x1, blocking collectives, local(): marginal = lax.psum(half, 'mkt')  12.6 us
    gather x1, local copies, waits for them, and re-layouts, local(): trade_rows_all = table[trade_block]  11 us
    another operation x1, loops' own time, local(): values = lax.map(price, jnp.arange(scen_count, dtype=jnp.int32))  10.9 us
    psum x1, blocking collectives, local(): lax.psum(-jnp.dot(weights, values, precision=lax.Precision.HIGHEST), 'scen')  10.4 us
  transfers between devices with their start and end apart: 1, of which 1 were waited for; matrix products, arithmetic and copies ran while one was open for 1% of the time, Pallas kernels for 0%

profile of v1, /device:TPU:0, one launch (start us, length us, event | category | flops | bytes accessed | tf_op | source)
XLA Modules:
  0.0 227.6 jit_solution(3356208711474794789)
XLA Ops:
  0.7 33.3 %while.12 = (s32[]{:T(128)}, bf16[64,512]{1,0:T(8,128)(2,1)}, s32[16,2]{0,1:T(2,128)S(1)}, bf16[16,64,128]{2,1,0:T(8,128)(2,1)S(1)}, s32[]{:T(128)}) while((s32[]{:T(128)}, bf16[64,512]{1,0:T(8,128)(2,1)}, s32[16,2]{0,1:T(2,128)S(1)}, bf16[16,64,128]{2,1,0:T(8,128)(2,1)S(1)}, s32[]{:T(128)}) %tuple.34), condition=%wide.while_cond, body=%wide.while_body.sunk | while | flops 2 | bytes 32865 | solution.py:20
  35.2 6.0 %all-to-all-start = ((bf16[16,4,2048]{2,0,1:T(8,128)(2,1)}), bf16[16,4,2048]{2,0,1:T(8,128)(2,1)S(1)}, u32[]{:S(2)}, u32[]{:S(2)}) async-start(bf16[16,4,2048]{2,0,1:T(8,128)(2,1)} %copy.14), calls=%async_computation | async-start | bytes 524288 | tf_op jit(solution)/shard_map/all_to_all | solution.py:26
  43.2 6.9 %all-to-all-done = bf16[16,4,2048]{2,0,1:T(8,128)(2,1)S(1)} async-done(((bf16[16,4,2048]{2,0,1:T(8,128)(2,1)}), bf16[16,4,2048]{2,0,1:T(8,128)(2,1)S(1)}, u32[]{:S(2)}, u32[]{:S(2)}) %all-to-all-start) | async-done | bytes 262176 | tf_op jit(solution)/shard_map/all_to_all | solution.py:26
  50.2 11.0 %gather_fusion = bf16[2048,2048]{1,0:T(8,128)(2,1)} fusion(bf16[64,2048]{1,0:T(8,128)(2,1)S(1)} %bitcast.38, s32[2048]{0:T(1024)S(1)} %fusion.6), kind=kCustom, calls=%fused_computation | custom fusion | bytes 16785408 | tf_op jit(solution)/shard_map/gather | solution.py:28
  61.2 101.0 %while.11 = (s32[]{:T(128)}, f32[16,2048]{1,0:T(8,128)S(1)}, s32[16]{0:T(128)S(1)}, bf16[2048,2048]{1,0:T(8,128)(2,1)}, bf16[128,256]{1,0:T(8,128)(2,1)S(1)}, /*...) while((s32[]{:T(128)}, f32[16,2048]{1,0:T(8,128)S(1)}, ...), condition=%wide.region_1.2_spmd, body=%wide.region_0.1_spmd.sunk | while | flops 409993216 | bytes 4942527 | solution.py:41
  62.5 2.8 %multiply_convert_fusion.3 = bf16[2048,256]{1,0:T(8,128)(2,1)} fusion(f32[2048,256]{1,0:T(8,128)S(1)} %get-tuple-element.213, bf16[128,256]{1,0:T(8,128)(2,1)S(1)} %get-tuple-element.212, bf16[2048,2048]{1,0:T(8,128)(2,1)} %get-tuple-element.211, s32[]{:T(128)S(6)} %select_n.23), kind=kOutput, calls=%fused_computation.4.clone.1 | convolution fusion | flops 137363456 | bytes 3735556 | tf_op jit(solution)/shard_map/while/body/eval_jaxpr/dot_general | solution.py:34
  68.8 2.8 %multiply_convert_fusion.3 = bf16[2048,256]{1,0:T(8,128)(2,1)} fusion(f32[2048,256]{1,0:T(8,128)S(1)} %get-tuple-element.213, bf16[128,256]{1,0:T(8,128)(2,1)S(1)} %get-tuple-element.212, bf16[2048,2048]{1,0:T(8,128)(2,1)} %get-tuple-element.211, s32[]{:T(128)S(6)} %select_n.23), kind=kOutput, calls=%fused_computation.4.clone.1 | convolution fusion | flops 137363456 | bytes 3735556 | tf_op jit(solution)/shard_map/while/body/eval_jaxpr/dot_general | solution.py:34
  71.6 2.0 fusion.29
  75.1 2.8 %multiply_convert_fusion.3 = bf16[2048,256]{1,0:T(8,128)(2,1)} fusion(f32[2048,256]{1,0:T(8,128)S(1)} %get-tuple-element.213, bf16[128,256]{1,0:T(8,128)(2,1)S(1)} %get-tuple-element.212, bf16[2048,2048]{1,0:T(8,128)(2,1)} %get-tuple-element.211, s32[]{:T(128)S(6)} %select_n.23), kind=kOutput, calls=%fused_computation.4.clone.1 | convolution fusion | flops 137363456 | bytes 3735556 | tf_op jit(solution)/shard_map/while/body/eval_jaxpr/dot_general | solution.py:34
  77.9 2.0 fusion.29
  81.4 2.8 %multiply_convert_fusion.3 = bf16[2048,256]{1,0:T(8,128)(2,1)} fusion(f32[2048,256]{1,0:T(8,128)S(1)} %get-tuple-element.213, bf16[128,256]{1,0:T(8,128)(2,1)S(1)} %get-tuple-element.212, bf16[2048,2048]{1,0:T(8,128)(2,1)} %get-tuple-element.211, s32[]{:T(128)S(6)} %select_n.23), kind=kOutput, calls=%fused_computation.4.clone.1 | convolution fusion | flops 137363456 | bytes 3735556 | tf_op jit(solution)/shard_map/while/body/eval_jaxpr/dot_general | solution.py:34
  84.2 2.0 fusion.29
  87.7 2.8 %multiply_convert_fusion.3 = bf16[2048,256]{1,0:T(8,128)(2,1)} fusion(f32[2048,256]{1,0:T(8,128)S(1)} %get-tuple-element.213, bf16[128,256]{1,0:T(8,128)(2,1)S(1)} %get-tuple-element.212, bf16[2048,2048]{1,0:T(8,128)(2,1)} %get-tuple-element.211, s32[]{:T(128)S(6)} %select_n.23), kind=kOutput, calls=%fused_computation.4.clone.1 | convolution fusion | flops 137363456 | bytes 3735556 | tf_op jit(solution)/shard_map/while/body/eval_jaxpr/dot_general | solution.py:34
  90.5 2.0 fusion.29
  94.0 2.8 %multiply_convert_fusion.3 = bf16[2048,256]{1,0:T(8,128)(2,1)} fusion(f32[2048,256]{1,0:T(8,128)S(1)} %get-tuple-element.213, bf16[128,256]{1,0:T(8,128)(2,1)S(1)} %get-tuple-element.212, bf16[2048,2048]{1,0:T(8,128)(2,1)} %get-tuple-element.211, s32[]{:T(128)S(6)} %select_n.23), kind=kOutput, calls=%fused_computation.4.clone.1 | convolution fusion | flops 137363456 | bytes 3735556 | tf_op jit(solution)/shard_map/while/body/eval_jaxpr/dot_general | solution.py:34
  96.8 2.0 fusion.29
  100.3 2.8 %multiply_convert_fusion.3 = bf16[2048,256]{1,0:T(8,128)(2,1)} fusion(f32[2048,256]{1,0:T(8,128)S(1)} %get-tuple-element.213, bf16[128,256]{1,0:T(8,128)(2,1)S(1)} %get-tuple-element.212, bf16[2048,2048]{1,0:T(8,128)(2,1)} %get-tuple-element.211, s32[]{:T(128)S(6)} %select_n.23), kind=kOutput, calls=%fused_computation.4.clone.1 | convolution fusion | flops 137363456 | bytes 3735556 | tf_op jit(solution)/shard_map/while/body/eval_jaxpr/dot_general | solution.py:34
  103.2 2.0 fusion.29
  106.6 2.8 %multiply_convert_fusion.3 = bf16[2048,256]{1,0:T(8,128)(2,1)} fusion(f32[2048,256]{1,0:T(8,128)S(1)} %get-tuple-element.213, bf16[128,256]{1,0:T(8,128)(2,1)S(1)} %get-tuple-element.212, bf16[2048,2048]{1,0:T(8,128)(2,1)} %get-tuple-element.211, s32[]{:T(128)S(6)} %select_n.23), kind=kOutput, calls=%fused_computation.4.clone.1 | convolution fusion | flops 137363456 | bytes 3735556 | tf_op jit(solution)/shard_map/while/body/eval_jaxpr/dot_general | solution.py:34
  109.5 2.0 fusion.29
  113.0 2.8 %multiply_convert_fusion.3 = bf16[2048,256]{1,0:T(8,128)(2,1)} fusion(f32[2048,256]{1,0:T(8,128)S(1)} %get-tuple-element.213, bf16[128,256]{1,0:T(8,128)(2,1)S(1)} %get-tuple-element.212, bf16[2048,2048]{1,0:T(8,128)(2,1)} %get-tuple-element.211, s32[]{:T(128)S(6)} %select_n.23), kind=kOutput, calls=%fused_computation.4.clone.1 | convolution fusion | flops 137363456 | bytes 3735556 | tf_op jit(solution)/shard_map/while/body/eval_jaxpr/dot_general | solution.py:34
  115.8 2.0 fusion.29
  119.3 2.8 %multiply_convert_fusion.3 = bf16[2048,256]{1,0:T(8,128)(2,1)} fusion(f32[2048,256]{1,0:T(8,128)S(1)} %get-tuple-element.213, bf16[128,256]{1,0:T(8,128)(2,1)S(1)} %get-tuple-element.212, bf16[2048,2048]{1,0:T(8,128)(2,1)} %get-tuple-element.211, s32[]{:T(128)S(6)} %select_n.23), kind=kOutput, calls=%fused_computation.4.clone.1 | convolution fusion | flops 137363456 | bytes 3735556 | tf_op jit(solution)/shard_map/while/body/eval_jaxpr/dot_general | solution.py:34
  125.6 2.8 %multiply_convert_fusion.3 = bf16[2048,256]{1,0:T(8,128)(2,1)} fusion(f32[2048,256]{1,0:T(8,128)S(1)} %get-tuple-element.213, bf16[128,256]{1,0:T(8,128)(2,1)S(1)} %get-tuple-element.212, bf16[2048,2048]{1,0:T(8,128)(2,1)} %get-tuple-element.211, s32[]{:T(128)S(6)} %select_n.23), kind=kOutput, calls=%fused_computation.4.clone.1 | convolution fusion | flops 137363456 | bytes 3735556 | tf_op jit(solution)/shard_map/while/body/eval_jaxpr/dot_general | solution.py:34
  131.9 2.8 %multiply_convert_fusion.3 = bf16[2048,256]{1,0:T(8,128)(2,1)} fusion(f32[2048,256]{1,0:T(8,128)S(1)} %get-tuple-element.213, bf16[128,256]{1,0:T(8,128)(2,1)S(1)} %get-tuple-element.212, bf16[2048,2048]{1,0:T(8,128)(2,1)} %get-tuple-element.211, s32[]{:T(128)S(6)} %select_n.23), kind=kOutput, calls=%fused_computation.4.clone.1 | convolution fusion | flops 137363456 | bytes 3735556 | tf_op jit(solution)/shard_map/while/body/eval_jaxpr/dot_general | solution.py:34
  138.2 2.8 %multiply_convert_fusion.3 = bf16[2048,256]{1,0:T(8,128)(2,1)} fusion(f32[2048,256]{1,0:T(8,128)S(1)} %get-tuple-element.213, bf16[128,256]{1,0:T(8,128)(2,1)S(1)} %get-tuple-element.212, bf16[2048,2048]{1,0:T(8,128)(2,1)} %get-tuple-element.211, s32[]{:T(128)S(6)} %select_n.23), kind=kOutput, calls=%fused_computation.4.clone.1 | convolution fusion | flops 137363456 | bytes 3735556 | tf_op jit(solution)/shard_map/while/body/eval_jaxpr/dot_general | solution.py:34
  144.5 2.8 %multiply_convert_fusion.3 = bf16[2048,256]{1,0:T(8,128)(2,1)} fusion(f32[2048,256]{1,0:T(8,128)S(1)} %get-tuple-element.213, bf16[128,256]{1,0:T(8,128)(2,1)S(1)} %get-tuple-element.212, bf16[2048,2048]{1,0:T(8,128)(2,1)} %get-tuple-element.211, s32[]{:T(128)S(6)} %select_n.23), kind=kOutput, calls=%fused_computation.4.clone.1 | convolution fusion | flops 137363456 | bytes 3735556 | tf_op jit(solution)/shard_map/while/body/eval_jaxpr/dot_general | solution.py:34
  150.8 2.8 %multiply_convert_fusion.3 = bf16[2048,256]{1,0:T(8,128)(2,1)} fusion(f32[2048,256]{1,0:T(8,128)S(1)} %get-tuple-element.213, bf16[128,256]{1,0:T(8,128)(2,1)S(1)} %get-tuple-element.212, bf16[2048,2048]{1,0:T(8,128)(2,1)} %get-tuple-element.211, s32[]{:T(128)S(6)} %select_n.23), kind=kOutput, calls=%fused_computation.4.clone.1 | convolution fusion | flops 137363456 | bytes 3735556 | tf_op jit(solution)/shard_map/while/body/eval_jaxpr/dot_general | solution.py:34
  157.1 2.8 %multiply_convert_fusion.3 = bf16[2048,256]{1,0:T(8,128)(2,1)} fusion(f32[2048,256]{1,0:T(8,128)S(1)} %get-tuple-element.213, bf16[128,256]{1,0:T(8,128)(2,1)S(1)} %get-tuple-element.212, bf16[2048,2048]{1,0:T(8,128)(2,1)} %get-tuple-element.211, s32[]{:T(128)S(6)} %select_n.23), kind=kOutput, calls=%fused_computation.4.clone.1 | convolution fusion | flops 137363456 | bytes 3735556 | tf_op jit(solution)/shard_map/while/body/eval_jaxpr/dot_general | solution.py:34
  165.7 38.8 %psum.26 = f32[]{:T(128)} all-reduce(f32[]{:T(128)S(6)} %neg.22), channel_id=1, replica_groups=mesh['mkt'=8,'trade'=1,'scen'=4] {'mkt','scen'}, use_global_device_ids=true, to_apply=%region_5.6 | all-reduce | flops 1 | bytes 8 | tf_op jit(solution)/shard_map/psum | solution.py:51
  204.6 10.4 %psum.24 = f32[2048]{0:T(1024)S(1)} all-reduce(f32[2048]{0:T(1024)S(1)} %neg.21), channel_id=1, replica_groups=mesh['mkt'=8,'trade'=1,'scen'=4] {'scen'}, use_global_device_ids=true, to_apply=%region_3.4 | all-reduce | flops 2048 | bytes 16384 | tf_op jit(solution)/shard_map/psum | solution.py:47
  215.0 12.6 %psum.25 = f32[2048]{0:T(1024)} all-reduce(f32[2048]{0:T(1024)S(1)} %psum.24), channel_id=1, replica_groups=mesh['mkt'=8,'trade'=1,'scen'=4] {'mkt'}, use_global_device_ids=true, to_apply=%region_4.5 | all-reduce | flops 2048 | bytes 16384 | tf_op jit(solution)/shard_map/psum | solution.py:48
  (134 shorter events, 68.0 us)
Async XLA Ops:
  0.6 33.4 %copy-start = (bf16[16,128,128]{2,1,0:T(8,128)(2,1)S(1)}, bf16[16,128,128]{2,1,0:T(8,128)(2,1)}, u32[]{:S(2)}) copy-start(bf16[16,128,128]{2,1,0:T(8,128)(2,1)} %param.13) | copy-start | bytes 1572868
  34.4 8.9 %copy-start.2 = (s32[2048]{0:T(1024)S(1)}, s32[2048]{0:T(1024)}, u32[]{:S(2)}) copy-start(s32[2048]{0:T(1024)} %param.14) | copy-start | bytes 24580
  35.2 14.9 %all-to-all-start = ((bf16[16,4,2048]{2,0,1:T(8,128)(2,1)}), bf16[16,4,2048]{2,0,1:T(8,128)(2,1)S(1)}, u32[]{:S(2)}, u32[]{:S(2)}) async-start(bf16[16,4,2048]{2,0,1:T(8,128)(2,1)} %copy.14), calls=%async_computation | async-start | bytes 524288 | tf_op jit(solution)/shard_map/all_to_all | solution.py:26
  50.1 11.0 %copy-start.4 = (bf16[256,256]{1,0:T(8,128)(2,1)S(1)}, bf16[256,256]{1,0:T(8,128)(2,1)}, u32[]{:S(2)}) copy-start(bf16[256,256]{1,0:T(8,128)(2,1)} %param.19) | copy-start | bytes 393220
  50.1 11.0 %copy-start.5 = (bf16[128,256]{1,0:T(8,128)(2,1)S(1)}, bf16[128,256]{1,0:T(8,128)(2,1)}, u32[]{:S(2)}) copy-start(bf16[128,256]{1,0:T(8,128)(2,1)} %param.18) | copy-start | bytes 196612
  50.1 11.0 %copy-start.6 = (f32[256]{0:T(256)S(1)}, f32[256]{0:T(256)}, u32[]{:S(2)}) copy-start(f32[256]{0:T(256)} %param.20) | copy-start | bytes 3076
  50.1 11.0 %copy-start.7 = (bf16[256]{0:T(256)(128)(2,1)S(1)}, bf16[256]{0:T(256)(128)(2,1)}, u32[]{:S(2)}) copy-start(bf16[256]{0:T(256)(128)(2,1)} %param.21) | copy-start | bytes 1540
  61.2 101.0 %copy-start.1 = (f32[2048]{0:T(1024)S(1)}, f32[2048]{0:T(1024)}, u32[]{:S(2)}) copy-start(f32[2048]{0:T(1024)} %param.16) | copy-start | bytes 24580
  61.2 101.0 %copy-start.3 = (s32[16]{0:T(128)S(1)}, s32[16]{0:T(128)}, u32[]{:S(2)}) copy-start(s32[16]{0:T(128)} %param.17) | copy-start | bytes 196
